TPU v7x, 32 devices: a whole 2x2x4 slice. The times are simulated.
32 devices in a mesh: grp: 4 (over z), au: 4 (over x, core), vert: 2 (over y).
Axes of the slice: x: 2, y: 2, z: 4, core: 2. Of those that a mesh axis runs over, the one named last changes fastest.
Arguments:
- visibility: float32 [8192, 2], P(('grp', 'au', 'vert')), may hold values from -6 to 6
- destination: int32 [8192, 1], P(('grp', 'au', 'vert')), may hold values from 0 to 7; in each aligned block of 256 rows (0 to 255, 256 to 511, ...) at most 128 rows name the same one
- tile_slot: int32 [8192], P(('grp', 'au', 'vert')), may hold values from 0 to 63
- offsets: int32 [8192, 2], P(('grp', 'au', 'vert')), may hold values from 0 to 120
- taper: float32 [8], replicated, may hold values from 0.2 to 1
Outputs:
- dirty_facet: float32 [512, 512], P(('grp', 'au', 'vert'))
Inputs may be any that keep to these rules, and one draw needn't show every extreme that they name: `destination`: among the rows of one device (aligned blocks of 256 rows) no grid block is named more than 128 times, and in some blocks one is named exactly 128 times. `tile_slot`: A tile number within the owning grid block. `offsets`: the kernel's 8 taps stay inside the tile.
All inputs are finite; a program needn't handle non-finite values.
Results may differ from a plain program's by a relative error of at most 0.0003.
Values sent between devices are 32-bit elements.
A program may use at most 64 MiB of HBM per device.

v0:
```python
import math

import jax
import jax.numpy as jnp
from jax import lax
from jax.sharding import PartitionSpec as P

TILE = 128
SUP = 8
ROWS_DEV = 2048
COLS_DEV = 512
IMG = 512


def matmul(factor_a, factor_b):
    return jnp.dot(
        factor_a, factor_b, precision=lax.Precision.HIGHEST, preferred_element_type=jnp.float32
    )


def phases(pixels, grid_cells, modulus):
    turn_count = pixels[:, None] * (grid_cells[None, :] - modulus // 2) % modulus
    angles = turn_count.astype(jnp.float32) * (2.0 * math.pi / modulus)
    return (jnp.cos(angles), jnp.sin(angles))


def spread(anchor, extent, taper):
    offset = jnp.arange(extent, dtype=jnp.int32)[None, :] - anchor[:, None]
    kernel = jnp.zeros(offset.shape, jnp.float32)
    for tap_index in range(taper.shape[0]):
        kernel = kernel + jnp.where(offset == tap_index, taper[tap_index], 0.0)
    return kernel


def body(visibility, destination, tile_slot, offsets, taper):
    n_rows = lax.axis_size("au")
    n_cols = lax.axis_size("vert")
    owners = n_rows * n_cols
    vis_count = visibility.shape[0]
    capacity = 4 * vis_count // owners
    target = destination[:, 0]
    onehot = (target[:, None] == jnp.arange(owners, dtype=jnp.int32)[None, :]).astype(jnp.int32)
    before = jnp.cumsum(onehot, axis=0) - onehot
    rank_in = jnp.sum(before * onehot, axis=1)
    position = target * capacity + rank_in
    packed = (tile_slot * TILE + offsets[:, 0]) * TILE + offsets[:, 1]
    payload = jnp.concatenate([visibility, packed[:, None].astype(jnp.float32)], axis=1)
    outgoing = jnp.zeros((owners * capacity, 3), jnp.float32).at[position].set(payload)
    incoming = lax.all_to_all(outgoing, ("au", "vert"), split_axis=0, concat_axis=0, tiled=True)
    slot_code = incoming[:, 2].astype(jnp.int32)
    tiles_across = COLS_DEV // TILE
    tile_index = slot_code // (TILE * TILE)
    row_anchor = tile_index // tiles_across * TILE + slot_code // TILE % TILE
    col_anchor = tile_index % tiles_across * TILE + slot_code % TILE
    row_kernel = spread(row_anchor, ROWS_DEV, taper)
    col_kernel = spread(col_anchor, COLS_DEV, taper)
    weighted = jnp.concatenate(
        [incoming[:, 0:1] * col_kernel, incoming[:, 1:2] * col_kernel], axis=1
    )
    gridded = lax.dot_general(
        row_kernel,
        weighted,
        (((0,), (0,)), ((), ())),
        precision=lax.Precision.HIGHEST,
        preferred_element_type=jnp.float32,
    )
    grid_re = gridded[:, :COLS_DEV]
    grid_im = gridded[:, COLS_DEV:]
    total_rows = ROWS_DEV * n_rows
    total_cols = COLS_DEV * n_cols
    row_share = ROWS_DEV
    first_row = lax.axis_index("au") * ROWS_DEV
    pixel_cols = jnp.arange(IMG, dtype=jnp.int32) - IMG // 2
    col_cells = lax.axis_index("vert") * COLS_DEV + jnp.arange(COLS_DEV, dtype=jnp.int32)
    cos_v, sin_v = phases(pixel_cols, col_cells, total_cols)
    part_re = matmul(grid_re, cos_v.T) - matmul(grid_im, sin_v.T)
    part_im = matmul(grid_re, sin_v.T) + matmul(grid_im, cos_v.T)
    row_cells = first_row + jnp.arange(row_share, dtype=jnp.int32)
    normalise = 1.0 / (SUP * math.sqrt(vis_count * lax.axis_size(("grp", "au", "vert"))))

    def facet_rows():
        pixel_rows = (
            jnp.arange(
                IMG // lax.axis_size(("grp", "au", "vert")) * lax.axis_size(("grp", "au", "vert")),
                dtype=jnp.int32,
            )
            - IMG // 2
        )
        cos_u, sin_u = phases(pixel_rows, row_cells, total_rows)
        return (matmul(cos_u, part_re) - matmul(sin_u, part_im)) * normalise

    return lax.psum_scatter(facet_rows(), ("grp", "au", "vert"), scatter_dimension=0, tiled=True)


def solution(mesh):
    return jax.shard_map(
        body,
        mesh=mesh,
        in_specs=(
            P(("grp", "au", "vert"), None),
            P(("grp", "au", "vert"), None),
            P(("grp", "au", "vert")),
            P(("grp", "au", "vert"), None),
            P(),
        ),
        out_specs=P(("grp", "au", "vert"), None),
        check_vma=False,
    )
```

profile of v0, /device:TPU:0, one launch (start us, length us, event | category | flops | bytes accessed | tf_op | source)
XLA Modules:
  0.0 311.4 jit_solution(14008861631853625649)
XLA Ops:
  6.5 0.8 fusion.144
  7.3 0.7 fusion.104
  8.0 0.6 reduce-window.6
  8.5 0.2 slice_reduce_fusion
  8.8 0.8 fusion.103
  9.6 0.7 compare_select_fusion.5
  10.3 0.7 add_convert_fusion
  10.9 0.7 pad_maximum_fusion
  11.6 0.1 copy.8
  11.8 1.3 scatter_custom_fusion
  13.1 0.8 copy.9
  13.9 5.2 %all-to-all-start = ((f32[8,128,3]{1,2,0:T(4,128)}), f32[8,128,3]{1,2,0:T(4,128)S(1)}, u32[]{:S(2)}, u32[]{:S(2)}) async-start(f32[8,128,3]{1,2,0:T(4,128)} %copy.9), calls=%async_computation | async-start | bytes 32768 | tf_op jit(solution)/shard_map/all_to_all | solution.py:49
  19.1 0.0 reduce-scatter.2.cloned.1.call-start
  19.1 1.6 fusion.145
  20.8 3.0 all-to-all-done
  23.8 0.1 fusion.105
  23.9 6.9 %fusion.93 = (f32[1024,512]{1,0:T(8,128)S(1)}, f32[1024,512]{1,0:T(8,128)S(1)}) fusion(f32[]{:T(128)} %bitcast.19, f32[]{:T(128)} %bitcast.18, f32[]{:T(128)} %bitcast.17, f32[]{:T(128)} %bitcast.16, f32[]{:T(128)} %bitcast.15, f32[]{:T(128)} %bitcast.14, f32[]{:T(128)} %bitcast.13, f32[]{:T(128)} %bitcast.12, s32[1024]{0:T(1024)S(1)} %bitcast.34, ...), kind=kLoop, calls=%fused_computation.90 | loop fusion | flops 13631488 | bytes 4206624 | tf_op jit(solution)/shard_map/mul | solution.py:58
  30.8 46.0 %fusion = f32[2048,1024]{1,0:T(8,128)S(1)} fusion(f32[1024,512]{1,0:T(8,128)S(1)} %get-tuple-element.10, f32[1024,512]{1,0:T(8,128)S(1)} %get-tuple-element.9, f32[]{:T(128)} %bitcast.19, f32[]{:T(128)} %bitcast.18, f32[]{:T(128)} %bitcast.17, f32[]{:T(128)} %bitcast.16, f32[]{:T(128)} %bitcast.15, f32[]{:T(128)} %bitcast.14, f32[]{:T(128)} %bitcast.13, ...), kind=kOutput, calls=%fused_computation.1 | convolution fusion | flops 25821184000 | bytes 12587040 | tf_op jit(solution)/shard_map/dot_general | solution.py:60
  76.8 11.2 %fusion.66 = f32[2048,512]{1,0:T(8,128)S(1)} fusion(f32[2048,1024]{1,0:T(8,128)S(1)} %fusion, s32[512]{0:T(512)S(1)} %get-tuple-element.21, s32[512]{0:T(512)S(1)} %get-tuple-element.22), kind=kOutput, calls=%fused_computation.65 | convolution fusion | flops 6446120960 | bytes 8392704 | tf_op jit(solution)/shard_map/dot_general | solution.py:16
  88.0 11.3 %fusion.62 = f32[2048,512]{1,0:T(8,128)S(1)} fusion(f32[2048,1024]{1,0:T(8,128)S(1)} %fusion, s32[512]{0:T(512)S(1)} %get-tuple-element.21, s32[512]{0:T(512)S(1)} %get-tuple-element.22), kind=kOutput, calls=%fused_computation.61 | convolution fusion | flops 6446120960 | bytes 8392704 | tf_op jit(solution)/shard_map/dot_general | solution.py:16
  99.3 11.5 %fusion.64 = f32[2048,512]{1,0:T(8,128)S(1)} fusion(f32[2048,1024]{1,0:T(8,128)S(1)} %fusion, s32[512]{0:T(512)S(1)} %get-tuple-element.21, s32[512]{0:T(512)S(1)} %get-tuple-element.22), kind=kOutput, calls=%fused_computation.63 | convolution fusion | flops 6446120960 | bytes 8392704 | tf_op jit(solution)/shard_map/dot_general | solution.py:16
  110.8 11.3 %fusion.68 = f32[2048,512]{1,0:T(8,128)S(1)} fusion(f32[2048,1024]{1,0:T(8,128)S(1)} %fusion, s32[512]{0:T(512)S(1)} %get-tuple-element.21, s32[512]{0:T(512)S(1)} %get-tuple-element.22), kind=kOutput, calls=%fused_computation.67 | convolution fusion | flops 6446120960 | bytes 8392704 | tf_op jit(solution)/shard_map/dot_general | solution.py:16
  122.1 22.8 %fusion.38 = f32[512,512]{1,0:T(8,128)S(1)} fusion(f32[2048,512]{1,0:T(8,128)S(1)} %fusion.66, f32[2048,512]{1,0:T(8,128)S(1)} %fusion.62, s32[2048]{0:T(1024)S(1)} %add_add_fusion, s32[512]{0:T(512)S(1)} %get-tuple-element.22), kind=kOutput, calls=%fused_computation.37 | convolution fusion | flops 6458179584 | bytes 9447424 | tf_op jit(solution)/shard_map/dot_general | solution.py:16
  145.0 23.3 %fusion.85 = f32[512,512]{1,0:T(8,128)} fusion(f32[512,512]{1,0:T(8,128)S(1)} %fusion.38, f32[2048,512]{1,0:T(8,128)S(1)} %fusion.68, f32[2048,512]{1,0:T(8,128)S(1)} %fusion.64, s32[2048]{0:T(1024)S(1)} %add_add_fusion, s32[512]{0:T(512)S(1)} %get-tuple-element.22), kind=kOutput, calls=%fused_computation.85 | convolution fusion | flops 6458703872 | bytes 10496000 | tf_op jit(solution)/shard_map/dot_general | solution.py:16
  168.3 0.0 reduce-scatter.2.cloned.1.call-update
  168.3 136.1 %reduce-scatter.2.cloned.1.call-done = f32[16,512]{1,0:T(8,128)} async-done(((f32[512,512]{1,0:T(8,128)}), f32[16,512]{1,0:T(8,128)}) %reduce-scatter.2.cloned.1.call-update) | async-done | bytes 32784 | tf_op jit(solution)/shard_map/reduce_scatter | solution.py:92
  (6 shorter events, 0.1 us)
Async XLA Ops:
  13.9 9.9 %all-to-all-start = ((f32[8,128,3]{1,2,0:T(4,128)}), f32[8,128,3]{1,2,0:T(4,128)S(1)}, u32[]{:S(2)}, u32[]{:S(2)}) async-start(f32[8,128,3]{1,2,0:T(4,128)} %copy.9), calls=%async_computation | async-start | bytes 32768 | tf_op jit(solution)/shard_map/all_to_all | solution.py:49
  19.1 285.3 %reduce-scatter.2.cloned.1.call-start = ((), (), s32[]{:S(2)}) async-start(), calls=%async_computation.2 | async-start | bytes 1081344 | tf_op jit(solution)/shard_map/reduce_scatter | solution.py:92
Sparse Core Ops, SparseCore 0:
  168.4 135.9 reduce-scatter.1
where the time goes:
time: 315 us; the launch traced here: 311 us
  waiting for transfers between devices  139 us (44%)
  matrix products  137 us (43%)
  between operations  13.7 us (4%)
  other arithmetic  11.1 us (4%)
  starting transfers between devices  5.27 us (2%)
  local copies, waits for them, and re-layouts  4.83 us (2%)
    reduce_scatter x1, waiting for transfers between devices, body(): lax.psum_scatter(facet_rows(), ('grp', 'au', 'vert'), scatter_dimension=0...  136 us
    dot_general x6, matrix products, matmul(): jnp.dot(factor_a, factor_b, precision=lax.Precision.HIGHEST, preferred_el...  91.5 us
    dot_general x1, matrix products, body(): lax.dot_general(row_kernel, weighted, (((0,), (0,)), ((), ())), precision...  46 us
    mul x1, other arithmetic, body(): incoming[:, 0:1] * col_kernel  6.86 us
  transfers between devices with their start and end apart: 2, of which 2 were waited for; matrix products, arithmetic and copies ran while one was open for 1% of the time, Pallas kernels for 0%

commit v1 on v0

v1 whole, which is shorter than its diff:
```python
import functools
import math

import jax
import jax.numpy as jnp
from jax import lax
from jax.experimental import pallas as pl
from jax.experimental.pallas import tpu as pltpu
from jax.sharding import PartitionSpec as P

TILE = 128
SUP = 8
ROWS_DEV = 2048
COLS_DEV = 512
IMG = 512
LANES = 128
AXES = ("grp", "au", "vert")
MESH = pl.DeviceIdType.MESH


def turn(angle):
    x = (angle - jnp.floor(angle + 0.5)) * (0.5 * math.pi)
    x2 = x * x
    s = x * (1.0 + x2 * (-1.0 / 6 + x2 * (1.0 / 120 + x2 * (-1.0 / 5040))))
    c = 1.0 + x2 * (-0.5 + x2 * (1.0 / 24 + x2 * (-1.0 / 720 + x2 * (1.0 / 40320))))
    s, c = 2.0 * s * c, 1.0 - 2.0 * s * s
    return 1.0 - 2.0 * s * s, 2.0 * s * c


def times(a, b):
    return a[0] * b[0] - a[1] * b[1], a[0] * b[1] + a[1] * b[0]


def halves(parts):
    high = [part.astype(jnp.bfloat16) for part in parts]
    low = [(part - h.astype(jnp.float32)).astype(jnp.bfloat16) for part, h in zip(parts, high)]
    return jnp.concatenate(high + low, axis=0)


def iota(shape, dim):
    return lax.broadcasted_iota(jnp.int32, shape, dim)


def kernel(sizes, rows, vis_ref, dest_ref, slot_ref, off_ref, taper_ref, out_ref,
           own, held, acc, send_sem, recv_sem):
    n_grp, n_au, n_vert = sizes
    count = n_grp * n_au * n_vert
    g, a, v = (lax.axis_index(name) for name in AXES)
    me = (g * n_au + a) * n_vert + v
    total_rows, total_cols = ROWS_DEV * n_au, COLS_DEV * n_vert
    vis_count = vis_ref.shape[1]

    def peer(step):
        index = lax.rem(me + step, count)
        return (
            index,
            (index // (n_au * n_vert), lax.rem(index // n_vert, n_au), lax.rem(index, n_vert)),
        )

    barrier = pltpu.get_barrier_semaphore()

    @pl.loop(1, count)
    def _(step):
        pl.semaphore_signal(barrier, inc=1, device_id=peer(step)[1], device_id_type=MESH)

    across = COLS_DEV // TILE
    dest, slot = dest_ref[...], slot_ref[...]
    row0 = dest // n_vert * ROWS_DEV + slot // across * TILE + off_ref[0:1, :]
    col0 = dest % n_vert * COLS_DEV + slot % across * TILE + off_ref[1:2, :]
    own[0:2, :] = vis_ref[...]
    own[2:3, :] = (row0 - total_rows // 2).astype(jnp.float32)
    own[3:4, :] = (col0 - total_cols // 2).astype(jnp.float32)

    pad = -(-rows // 16) * 16
    blocks = IMG // LANES
    half = LANES // 2
    pixel_row = (me * rows - IMG // 2 + iota((pad, 1), 0)).astype(jnp.float32)
    tap_u = iota((pad, LANES), 1)
    tap_v = iota((SUP, IMG), 0)
    weight_u = jnp.zeros(tap_u.shape, jnp.float32)
    weight_v = jnp.zeros(tap_v.shape, jnp.float32)
    for tap in range(SUP):
        weight_u = jnp.where(tap_u == tap, taper_ref[tap], weight_u)
        weight_v = jnp.where(tap_v == tap, taper_ref[tap], weight_v)
    scale = 1.0 / (SUP * math.sqrt(vis_count * count))
    cos_u, sin_u = turn(pixel_row * tap_u.astype(jnp.float32) * (1.0 / total_rows))
    gain_u = (
        jnp.sum(weight_u * cos_u, axis=1, keepdims=True) * scale,
        jnp.sum(weight_u * sin_u, axis=1, keepdims=True) * scale,
    )
    pixel_col = (iota((SUP, IMG), 1) - IMG // 2).astype(jnp.float32)
    cos_v, sin_v = turn(pixel_col * tap_v.astype(jnp.float32) * (1.0 / total_cols))
    gain_v = (
        jnp.sum(weight_v * cos_v, axis=0, keepdims=True),
        jnp.sum(weight_v * sin_v, axis=0, keepdims=True),
    )
    eight = iota((8, 1), 0).astype(jnp.float32)
    centre = eight * LANES + (half - 0.5 - IMG // 2)

    pl.semaphore_wait(barrier, count - 1)

    def copy(slot_index, device, step):
        return pltpu.make_async_remote_copy(
            src_ref=own,
            dst_ref=held.at[slot_index],
            send_sem=send_sem.at[step],
            recv_sem=recv_sem.at[slot_index],
            device_id=device,
            device_id_type=MESH,
        )

    @pl.loop(1, count)
    def _(step):
        copy(me, peer(step)[1], step).start()

    def product(block):
        x, y = block[2:3, :], block[3:4, :]
        wave = times(turn(pixel_row * x * (1.0 / total_rows)), gain_u)
        wave = times(wave, (block[0:1, :], block[1:2, :]))
        y = y * (1.0 / total_cols)
        coarse = turn(centre * y)
        fine = turn((eight + 0.5) * y)
        steps = turn(8.0 * eight * y)
        left = [
            times(wave, (coarse[0][j : j + 1, :], coarse[1][j : j + 1, :])) for j in range(blocks)
        ]
        right = [
            times(fine, (steps[0][m : m + 1, :], steps[1][m : m + 1, :])) for m in range(half // 8)
        ]
        left = [jnp.concatenate([part[i] for part in left], axis=0) for i in (0, 1)]
        right = [jnp.concatenate([part[i] for part in right], axis=0) for i in (0, 1)]
        return lax.dot_general(
            halves(left),
            halves(right),
            (((1,), (1,)), ((), ())),
            preferred_element_type=jnp.float32,
        )

    acc[...] = product(own[...])

    @pl.loop(1, count)
    def _(step):
        source, device = peer(count - step)
        copy(source, device, step).wait_recv()
        acc[...] += product(held[source])

    top = blocks * pad
    folded = acc[: 2 * top, :] + acc[2 * top :, :]
    folded = folded[:, :LANES] + folded[:, LANES:]
    k, c = iota((LANES, LANES), 0), iota((LANES, LANES), 1)
    kk = lax.rem(k, half)
    plus = jnp.where(c == half + kk, 1.0, 0.0)
    minus = jnp.where(c == half - 1 - kk, 1.0, 0.0)
    even = jnp.where(k < half, plus + minus, 0.0)
    odd = jnp.where(k < half, 0.0, plus - minus)

    def dot(first, second):
        return jnp.dot(
            first, second, precision=lax.Precision.HIGHEST, preferred_element_type=jnp.float32
        )

    re, im = folded[:top, :], folded[top:, :]
    z_re = dot(re, even) - dot(im, odd)
    z_im = dot(im, even) + dot(re, odd)
    for j in range(blocks):
        span = slice(j * LANES, (j + 1) * LANES)
        tile = (
            z_re[j * pad : (j + 1) * pad, :] * gain_v[0][:, span]
            - z_im[j * pad : (j + 1) * pad, :] * gain_v[1][:, span]
        )
        out_ref[:, span] = tile[:rows, :]

    @pl.loop(1, count)
    def _(step):
        copy(me, peer(step)[1], step).wait_send()


def body(sizes, visibility, destination, tile_slot, offsets, taper):
    count = math.prod(sizes)
    vis_count = visibility.shape[0]
    rows = IMG // count
    pad = -(-rows // 16) * 16
    vmem = pl.BlockSpec(memory_space=pltpu.VMEM)
    return pl.pallas_call(
        functools.partial(kernel, sizes, rows),
        out_shape=jax.ShapeDtypeStruct((rows, IMG), jnp.float32),
        in_specs=[vmem] * 4 + [pl.BlockSpec(memory_space=pltpu.SMEM)],
        out_specs=vmem,
        scratch_shapes=[
            pltpu.VMEM((4, vis_count), jnp.float32),
            pltpu.VMEM((count, 4, vis_count), jnp.float32),
            pltpu.VMEM((4 * (IMG // LANES) * pad, 2 * LANES), jnp.float32),
            pltpu.SemaphoreType.DMA((count,)),
            pltpu.SemaphoreType.DMA((count,)),
        ],
        compiler_params=pltpu.CompilerParams(collective_id=0, has_side_effects=True),
        name="direct_facet",
    )(
        visibility.T,
        destination.reshape(1, vis_count),
        tile_slot.reshape(1, vis_count),
        offsets.T,
        taper,
    )


def solution(mesh):
    return jax.shard_map(
        functools.partial(body, tuple(mesh.shape[name] for name in AXES)),
        mesh=mesh,
        in_specs=(P(AXES, None), P(AXES, None), P(AXES), P(AXES, None), P()),
        out_specs=P(AXES, None),
        check_vma=False,
    )
```

time: 315 us -> 21.4 us (0.07); the launches traced: 311 us -> 21.2 us
  waiting for transfers between devices: 139 us -> 0 us
  matrix products: 137 us -> 0 us
  Pallas kernels: 0 us -> 19.8 us
  between operations: 13.7 us -> 0.01 us
  other arithmetic: 11.1 us -> 0 us
  starting transfers between devices: 5.27 us -> 0 us
  local copies, waits for them, and re-layouts: 4.83 us -> 1.38 us
    dot_general x7 -> x0, matrix products: 137 us -> none  [the longest x6 91.5 us: matmul(): jnp.dot(factor_a, factor_b, precision=lax.Precision.HIGHEST, preferred_el...]
    reduce_scatter x1 -> x0, waiting for transfers between devices: 136 us -> none  [body(): lax.psum_scatter(facet_rows(), ('grp', 'au', 'vert'), scatter_dimension=0...]
    pallas_call x0 -> x1, Pallas kernels: none -> 19.8 us  [body(): pl.pallas_call(functools.partial(kernel, sizes, rows), out_shape=jax.Shap...]
    mul x1 -> x0, other arithmetic: 6.86 us -> none  [body(): incoming[:, 0:1] * col_kernel]
    all_to_all x1 -> x0, starting transfers between devices: 5.23 us -> none  [body(): lax.all_to_all(outgoing, ('au', 'vert'), split_axis=0, concat_axis=0, til...]
  transfers between devices with their start and end apart: 2 -> 0, of which waited for: 2 -> 0; matrix products, arithmetic and copies ran while one was open for 1% -> 0% of each run, Pallas kernels for 0% -> 0%
where the time goes in v1:
time: 21.4 us; the launch traced here: 21.2 us
  Pallas kernels  19.8 us (93%)
  local copies, waits for them, and re-layouts  1.38 us (6%)
    pallas_call x1, Pallas kernels, body(): pl.pallas_call(functools.partial(kernel, sizes, rows), out_shape=jax.Shap...  19.8 us
    unnamed x1, local copies, waits for them, and re-layouts  1.38 us

profile of v1, /device:TPU:0, one launch (start us, length us, event | category | flops | bytes accessed | tf_op | source)
XLA Modules:
  0.0 21.2 jit_solution(2925177714300257213)
XLA Ops:
  0.0 19.8 %direct_facet.1 = f32[16,512]{1,0:T(8,128)} custom-call(f32[2,256]{1,0:T(2,128)} %bitcast.4, s32[1,256]{1,0:T(1,128)} %bitcast.6, s32[1,256]{1,0:T(1,128)} %bitcast.7, s32[2,256]{1,0:T(2,128)} %bitcast.5, f32[8]{0:T(128)} %taper_ref.1), custom_call_target="tpu_custom_call" | custom-call | tf_op jit(solution)/shard_map/direct_facet/pallas_call | solution.py:184
  19.9 1.4 %copy.7 = f32[16,512]{1,0:T(8,128)} copy(f32[16,512]{1,0:T(8,128)} %direct_facet.1) | data formatting | bytes 65536

commit v2 on v1

--- a/solution.py
+++ b/solution.py
@@ -41,8 +41,31 @@
     return lax.broadcasted_iota(jnp.int32, shape, dim)
 
 
-def kernel(sizes, rows, vis_ref, dest_ref, slot_ref, off_ref, taper_ref, out_ref,
-           own, held, acc, send_sem, recv_sem):
+def offsets_near_first(sizes):
+    n_grp, n_au, n_vert = sizes
+    cores = 2 if n_au % 2 == 0 else 1
+    ring = sorted(range(n_grp), key=lambda s: min(s, n_grp - s))
+    return [
+        (s_grp, s_chip, s_vert, s_core)
+        for s_grp in ring
+        for s_chip in range(n_au // cores)
+        for s_vert in range(n_vert)
+        for s_core in range(cores)
+    ]
+
+
+def arrival_groups(sizes):
+    plane = sizes[1] * sizes[2]
+    bounds = [1]
+    while bounds[-1] * 2 < plane:
+        bounds.append(bounds[-1] * 2)
+    bounds += [plane * k for k in range(1, sizes[0] + 1)]
+    bounds = sorted(set(bounds))
+    return list(zip(bounds[:-1], bounds[1:]))
+
+
+def kernel(sizes, rows, vis_hbm, dest_hbm, slot_hbm, off_hbm, taper_hbm, out_ref,
+           vis_ref, dest_ref, slot_ref, off_ref, taper_ref, held, acc, load_sem, send_sem, recv_sem):
     n_grp, n_au, n_vert = sizes
     count = n_grp * n_au * n_vert
     g, a, v = (lax.axis_index(name) for name in AXES)
@@ -50,26 +73,46 @@
     total_rows, total_cols = ROWS_DEV * n_au, COLS_DEV * n_vert
     vis_count = vis_ref.shape[1]
 
-    def peer(step):
-        index = lax.rem(me + step, count)
-        return (
-            index,
-            (index // (n_au * n_vert), lax.rem(index // n_vert, n_au), lax.rem(index, n_vert)),
-        )
+    loads = [
+        pltpu.make_async_copy(src, dst, load_sem.at[i])
+        for i, (src, dst) in enumerate(
+            [
+                (vis_hbm, vis_ref),
+                (dest_hbm, dest_ref),
+                (slot_hbm, slot_ref),
+                (off_hbm, off_ref),
+                (taper_hbm, taper_ref),
+            ]
+        )
+    ]
+    for load in loads:
+        load.start()
+
+    cores = 2 if n_au % 2 == 0 else 1
+    chips = n_au // cores
+    chip, core = a // cores, lax.rem(a, cores)
+    to_grp = [lax.rem(g + s, n_grp) for s in range(n_grp)]
+    to_chip = [lax.rem(chip + s, chips) * cores for s in range(chips)]
+    to_core = [lax.rem(core + s, cores) for s in range(cores)]
+    to_vert = [lax.rem(v + s, n_vert) for s in range(n_vert)]
+    peers = [
+        (to_grp[s_grp], to_chip[s_chip] + to_core[s_core], to_vert[s_vert])
+        for s_grp, s_chip, s_vert, s_core in offsets_near_first(sizes)
+    ]
 
     barrier = pltpu.get_barrier_semaphore()
-
-    @pl.loop(1, count)
-    def _(step):
-        pl.semaphore_signal(barrier, inc=1, device_id=peer(step)[1], device_id_type=MESH)
+    for peer in peers[:0:-1]:
+        pl.semaphore_signal(barrier, inc=1, device_id=peer, device_id_type=MESH)
+    for load in loads:
+        load.wait()
 
     across = COLS_DEV // TILE
     dest, slot = dest_ref[...], slot_ref[...]
     row0 = dest // n_vert * ROWS_DEV + slot // across * TILE + off_ref[0:1, :]
     col0 = dest % n_vert * COLS_DEV + slot % across * TILE + off_ref[1:2, :]
-    own[0:2, :] = vis_ref[...]
-    own[2:3, :] = (row0 - total_rows // 2).astype(jnp.float32)
-    own[3:4, :] = (col0 - total_cols // 2).astype(jnp.float32)
+    held[0, 0:2, :] = vis_ref[...]
+    held[0, 2:3, :] = (row0 - total_rows // 2).astype(jnp.float32)
+    held[0, 3:4, :] = (col0 - total_cols // 2).astype(jnp.float32)
 
     pad = -(-rows // 16) * 16
     blocks = IMG // LANES
@@ -94,39 +137,44 @@
         jnp.sum(weight_v * cos_v, axis=0, keepdims=True),
         jnp.sum(weight_v * sin_v, axis=0, keepdims=True),
     )
-    eight = iota((8, 1), 0).astype(jnp.float32)
-    centre = eight * LANES + (half - 0.5 - IMG // 2)
+    eight = iota((8, 1), 0)
+    fine_row = eight.astype(jnp.float32) + 0.5
+    centre = (eight * LANES).astype(jnp.float32) + (half - 0.5 - IMG // 2)
+    stride = 8.0 * (eight - (blocks - 1)).astype(jnp.float32)
+    mixed_row = jnp.where(eight < blocks, centre, stride)
 
     pl.semaphore_wait(barrier, count - 1)
 
-    def copy(slot_index, device, step):
-        return pltpu.make_async_remote_copy(
-            src_ref=own,
-            dst_ref=held.at[slot_index],
-            send_sem=send_sem.at[step],
-            recv_sem=recv_sem.at[slot_index],
-            device_id=device,
-            device_id_type=MESH,
-        )
-
-    @pl.loop(1, count)
-    def _(step):
-        copy(me, peer(step)[1], step).start()
+    groups = arrival_groups(sizes)
+    for number, (first, last) in reversed(list(enumerate(groups))):
+        for index in range(first, last):
+            pltpu.make_async_remote_copy(
+                src_ref=held.at[0],
+                dst_ref=held.at[index],
+                send_sem=send_sem,
+                recv_sem=recv_sem.at[number],
+                device_id=peers[index],
+                device_id_type=MESH,
+            ).start()
+
+    def landed(first, last, sem):
+        span = held.at[pl.ds(first, last - first)]
+        return pltpu.make_async_copy(span, span, sem)
 
     def product(block):
         x, y = block[2:3, :], block[3:4, :]
         wave = times(turn(pixel_row * x * (1.0 / total_rows)), gain_u)
         wave = times(wave, (block[0:1, :], block[1:2, :]))
         y = y * (1.0 / total_cols)
-        coarse = turn(centre * y)
-        fine = turn((eight + 0.5) * y)
-        steps = turn(8.0 * eight * y)
-        left = [
-            times(wave, (coarse[0][j : j + 1, :], coarse[1][j : j + 1, :])) for j in range(blocks)
-        ]
-        right = [
-            times(fine, (steps[0][m : m + 1, :], steps[1][m : m + 1, :])) for m in range(half // 8)
-        ]
+        mixed = turn(mixed_row * y)
+
+        def row(j):
+            return mixed[0][j : j + 1, :], mixed[1][j : j + 1, :]
+
+        left = [times(wave, row(j)) for j in range(blocks)]
+        right = [turn(fine_row * y)]
+        right += [times(right[0], row(j)) for j in range(blocks, 7)]
+        right += [times(part, row(7)) for part in right]
         left = [jnp.concatenate([part[i] for part in left], axis=0) for i in (0, 1)]
         right = [jnp.concatenate([part[i] for part in right], axis=0) for i in (0, 1)]
         return lax.dot_general(
@@ -136,13 +184,17 @@
             preferred_element_type=jnp.float32,
         )
 
-    acc[...] = product(own[...])
-
-    @pl.loop(1, count)
-    def _(step):
-        source, device = peer(count - step)
-        copy(source, device, step).wait_recv()
-        acc[...] += product(held[source])
+    acc[...] = jnp.zeros_like(acc)
+
+    @pl.loop(0, count // 2)
+    def _(pair):
+        for number, (first, last) in enumerate(groups):
+
+            @pl.when(pair == first // 2)
+            def _():
+                landed(first, last, recv_sem.at[number]).wait()
+
+        acc[...] += product(jnp.concatenate([held[2 * pair], held[2 * pair + 1]], axis=1))
 
     top = blocks * pad
     folded = acc[: 2 * top, :] + acc[2 * top :, :]
@@ -170,9 +222,7 @@
         )
         out_ref[:, span] = tile[:rows, :]
 
-    @pl.loop(1, count)
-    def _(step):
-        copy(me, peer(step)[1], step).wait_send()
+    landed(1, count, send_sem).wait()
 
 
 def body(sizes, visibility, destination, tile_slot, offsets, taper):
@@ -184,14 +234,19 @@
     return pl.pallas_call(
         functools.partial(kernel, sizes, rows),
         out_shape=jax.ShapeDtypeStruct((rows, IMG), jnp.float32),
-        in_specs=[vmem] * 4 + [pl.BlockSpec(memory_space=pltpu.SMEM)],
+        in_specs=[pl.BlockSpec(memory_space=pl.ANY)] * 5,
         out_specs=vmem,
         scratch_shapes=[
-            pltpu.VMEM((4, vis_count), jnp.float32),
+            pltpu.VMEM((2, vis_count), jnp.float32),
+            pltpu.VMEM((1, vis_count), jnp.int32),
+            pltpu.VMEM((1, vis_count), jnp.int32),
+            pltpu.VMEM((2, vis_count), jnp.int32),
+            pltpu.SMEM((SUP,), jnp.float32),
             pltpu.VMEM((count, 4, vis_count), jnp.float32),
             pltpu.VMEM((4 * (IMG // LANES) * pad, 2 * LANES), jnp.float32),
-            pltpu.SemaphoreType.DMA((count,)),
-            pltpu.SemaphoreType.DMA((count,)),
+            pltpu.SemaphoreType.DMA((5,)),
+            pltpu.SemaphoreType.DMA,
+            pltpu.SemaphoreType.DMA((len(arrival_groups(sizes)),)),
         ],
         compiler_params=pltpu.CompilerParams(collective_id=0, has_side_effects=True),
         name="direct_facet",

time: 21.4 us -> 17.7 us (0.83)
  Pallas kernels: 19.8 us -> 16.1 us
    pallas_call x1, Pallas kernels: 19.8 us -> 16.1 us  [body(): pl.pallas_call(functools.partial(kernel, sizes, rows), out_shape=jax.Shap...]
where the time goes in v2:
time: 17.7 us; the launch traced here: 17.5 us
  Pallas kernels  16.1 us (91%)
  local copies, waits for them, and re-layouts  1.38 us (8%)
    pallas_call x1, Pallas kernels, body(): pl.pallas_call(functools.partial(kernel, sizes, rows), out_shape=jax.Shap...  16.1 us
    unnamed x1, local copies, waits for them, and re-layouts  1.38 us

profile of v2, /device:TPU:0, one launch (start us, length us, event | category | flops | bytes accessed | tf_op | source)
XLA Modules:
  0.0 17.5 jit_solution(3960288606413062039)
XLA Ops:
  0.0 16.1 %direct_facet.1 = f32[16,512]{1,0:T(8,128)} custom-call(f32[2,256]{1,0:T(2,128)} %bitcast.4, s32[1,256]{1,0:T(1,128)} %bitcast.6, s32[1,256]{1,0:T(1,128)} %bitcast.7, s32[2,256]{1,0:T(2,128)} %bitcast.5, f32[8]{0:T(128)} %taper_hbm.1), custom_call_target="tpu_custom_call" | custom-call | tf_op jit(solution)/shard_map/direct_facet/pallas_call | solution.py:234
  16.1 1.4 %copy.7 = f32[16,512]{1,0:T(8,128)} copy(f32[16,512]{1,0:T(8,128)} %direct_facet.1) | data formatting | bytes 65536

commit v3 on v2

--- a/solution.py
+++ b/solution.py
@@ -21,8 +21,8 @@
 def turn(angle):
     x = (angle - jnp.floor(angle + 0.5)) * (0.5 * math.pi)
     x2 = x * x
-    s = x * (1.0 + x2 * (-1.0 / 6 + x2 * (1.0 / 120 + x2 * (-1.0 / 5040))))
-    c = 1.0 + x2 * (-0.5 + x2 * (1.0 / 24 + x2 * (-1.0 / 720 + x2 * (1.0 / 40320))))
+    s = x * (0.999994998 + x2 * (-0.166601620 + x2 * 0.008121558))
+    c = 0.999999972 + x2 * (-0.499998567 + x2 * (0.041655027 + x2 * (-0.001358591)))
     s, c = 2.0 * s * c, 1.0 - 2.0 * s * s
     return 1.0 - 2.0 * s * s, 2.0 * s * c
 
@@ -65,7 +65,7 @@
 
 
 def kernel(sizes, rows, vis_hbm, dest_hbm, slot_hbm, off_hbm, taper_hbm, out_ref,
-           vis_ref, dest_ref, slot_ref, off_ref, taper_ref, held, acc, load_sem, send_sem, recv_sem):
+           vis_ref, dest_ref, slot_ref, off_ref, taper_ref, held, lhs, rhs, acc, load_sem, send_sem, recv_sem):
     n_grp, n_au, n_vert = sizes
     count = n_grp * n_au * n_vert
     g, a, v = (lax.axis_index(name) for name in AXES)
@@ -138,10 +138,50 @@
         jnp.sum(weight_v * sin_v, axis=0, keepdims=True),
     )
     eight = iota((8, 1), 0)
+    k, c = iota((LANES, LANES), 0), iota((LANES, LANES), 1)
+    kk = lax.rem(k, half)
+    plus = jnp.where(c == half + kk, 1.0, 0.0)
+    minus = jnp.where(c == half - 1 - kk, 1.0, 0.0)
+    even = jnp.where(k < half, plus + minus, 0.0)
+    odd = jnp.where(k < half, 0.0, plus - minus)
     fine_row = eight.astype(jnp.float32) + 0.5
     centre = (eight * LANES).astype(jnp.float32) + (half - 0.5 - IMG // 2)
-    stride = 8.0 * (eight - (blocks - 1)).astype(jnp.float32)
-    mixed_row = jnp.where(eight < blocks, centre, stride)
+    mixed_v = jnp.where(eight == 4, 8.0, jnp.where(eight == 5, 16.0, 32.0))
+    mixed_v = jnp.where(eight < blocks, centre, jnp.where(eight == 7, 0.0, mixed_v))
+    mixed_u = jnp.where(eight == 7, 8.0, 0.0)
+
+    def fill(buffer, part, block):
+        x = block[2:3, :] * (1.0 / total_rows)
+        y = block[3:4, :] * (1.0 / total_cols)
+        mixed = turn(mixed_v * y + mixed_u * x)
+        seeded = times(mixed, (block[0:1, :], block[1:2, :]))
+
+        def row(pair, j):
+            return pair[0][j : j + 1, :], pair[1][j : j + 1, :]
+
+        waves = [turn(pixel_row[:8] * x)]
+        for _ in range(1, pad // 8):
+            waves.append(times(waves[-1], row(mixed, 7)))
+        left = [times(wave, row(seeded, j)) for j in range(blocks) for wave in waves]
+        right = [turn(fine_row * y)]
+        for j in (4, 5, 6):
+            right += [times(piece, row(mixed, j)) for piece in right]
+        left = [jnp.concatenate([piece[i] for piece in left], axis=0) for i in (0, 1)]
+        right = [jnp.concatenate([piece[i] for piece in right], axis=0) for i in (0, 1)]
+        span = slice(part * vis_count, (part + 1) * vis_count)
+        lhs[buffer, :, span] = halves(left)
+        rhs[buffer, :, span] = halves(right)
+
+    def product(buffer):
+        acc[...] += lax.dot_general(
+            lhs[buffer],
+            rhs[buffer],
+            (((1,), (1,)), ((), ())),
+            preferred_element_type=jnp.float32,
+        )
+
+    acc[...] = jnp.zeros_like(acc)
+    fill(0, 0, held[0])
 
     pl.semaphore_wait(barrier, count - 1)
 
@@ -161,65 +201,48 @@
         span = held.at[pl.ds(first, last - first)]
         return pltpu.make_async_copy(span, span, sem)
 
-    def product(block):
-        x, y = block[2:3, :], block[3:4, :]
-        wave = times(turn(pixel_row * x * (1.0 / total_rows)), gain_u)
-        wave = times(wave, (block[0:1, :], block[1:2, :]))
-        y = y * (1.0 / total_cols)
-        mixed = turn(mixed_row * y)
-
-        def row(j):
-            return mixed[0][j : j + 1, :], mixed[1][j : j + 1, :]
-
-        left = [times(wave, row(j)) for j in range(blocks)]
-        right = [turn(fine_row * y)]
-        right += [times(right[0], row(j)) for j in range(blocks, 7)]
-        right += [times(part, row(7)) for part in right]
-        left = [jnp.concatenate([part[i] for part in left], axis=0) for i in (0, 1)]
-        right = [jnp.concatenate([part[i] for part in right], axis=0) for i in (0, 1)]
-        return lax.dot_general(
-            halves(left),
-            halves(right),
-            (((1,), (1,)), ((), ())),
-            preferred_element_type=jnp.float32,
-        )
-
-    acc[...] = jnp.zeros_like(acc)
-
-    @pl.loop(0, count // 2)
-    def _(pair):
+    def arrive(pair):
         for number, (first, last) in enumerate(groups):
+            if first == 1:
+                continue
 
             @pl.when(pair == first // 2)
             def _():
                 landed(first, last, recv_sem.at[number]).wait()
 
-        acc[...] += product(jnp.concatenate([held[2 * pair], held[2 * pair + 1]], axis=1))
+    def advance(pair, buffer):
+        arrive(pair)
+        product(1 - buffer)
+        fill(buffer, 0, held[2 * pair])
+        fill(buffer, 1, held[2 * pair + 1])
+
+    landed(1, 2, recv_sem.at[0]).wait()
+    fill(0, 1, held[1])
+
+    @pl.loop(0, count // 4 - 1)
+    def _(quad):
+        advance(2 * quad + 1, 1)
+        advance(2 * quad + 2, 0)
+
+    advance(count // 2 - 1, 1)
+    product(1)
 
     top = blocks * pad
     folded = acc[: 2 * top, :] + acc[2 * top :, :]
     folded = folded[:, :LANES] + folded[:, LANES:]
-    k, c = iota((LANES, LANES), 0), iota((LANES, LANES), 1)
-    kk = lax.rem(k, half)
-    plus = jnp.where(c == half + kk, 1.0, 0.0)
-    minus = jnp.where(c == half - 1 - kk, 1.0, 0.0)
-    even = jnp.where(k < half, plus + minus, 0.0)
-    odd = jnp.where(k < half, 0.0, plus - minus)
-
     def dot(first, second):
         return jnp.dot(
             first, second, precision=lax.Precision.HIGHEST, preferred_element_type=jnp.float32
         )
 
-    re, im = folded[:top, :], folded[top:, :]
-    z_re = dot(re, even) - dot(im, odd)
-    z_im = dot(im, even) + dot(re, odd)
+    evens, odds = dot(folded, even), dot(folded, odd)
+    z_re = evens[:top, :] - odds[top:, :]
+    z_im = evens[top:, :] + odds[:top, :]
     for j in range(blocks):
         span = slice(j * LANES, (j + 1) * LANES)
-        tile = (
-            z_re[j * pad : (j + 1) * pad, :] * gain_v[0][:, span]
-            - z_im[j * pad : (j + 1) * pad, :] * gain_v[1][:, span]
-        )
+        here = slice(j * pad, (j + 1) * pad)
+        z = times((z_re[here, :], z_im[here, :]), gain_u)
+        tile = z[0] * gain_v[0][:, span] - z[1] * gain_v[1][:, span]
         out_ref[:, span] = tile[:rows, :]
 
     landed(1, count, send_sem).wait()
@@ -243,6 +266,8 @@
             pltpu.VMEM((2, vis_count), jnp.int32),
             pltpu.SMEM((SUP,), jnp.float32),
             pltpu.VMEM((count, 4, vis_count), jnp.float32),
+            pltpu.VMEM((2, 4 * (IMG // LANES) * pad, 2 * vis_count), jnp.bfloat16),
+            pltpu.VMEM((2, 2 * LANES, 2 * vis_count), jnp.bfloat16),
             pltpu.VMEM((4 * (IMG // LANES) * pad, 2 * LANES), jnp.float32),
             pltpu.SemaphoreType.DMA((5,)),
             pltpu.SemaphoreType.DMA,

time: 17.7 us -> 17.5 us (0.989)
  no operation moved by 1% of the time
where the time goes in v3:
time: 17.5 us; the launch traced here: 17.3 us
  Pallas kernels  16 us (91%)
  local copies, waits for them, and re-layouts  1.38 us (8%)
    pallas_call x1, Pallas kernels, body(): pl.pallas_call(functools.partial(kernel, sizes, rows), out_shape=jax.Shap...  16 us
    unnamed x1, local copies, waits for them, and re-layouts  1.38 us

profile of v3, /device:TPU:0, one launch (start us, length us, event | category | flops | bytes accessed | tf_op | source)
XLA Modules:
  0.0 17.3 jit_solution(16843026204130128905)
XLA Ops:
  0.0 16.0 %direct_facet.1 = f32[16,512]{1,0:T(8,128)} custom-call(f32[2,256]{1,0:T(2,128)} %bitcast.4, s32[1,256]{1,0:T(1,128)} %bitcast.6, s32[1,256]{1,0:T(1,128)} %bitcast.7, s32[2,256]{1,0:T(2,128)} %bitcast.5, f32[8]{0:T(128)} %taper_hbm.1), custom_call_target="tpu_custom_call" | custom-call | tf_op jit(solution)/shard_map/direct_facet/pallas_call | solution.py:257
  16.0 1.4 %copy.7 = f32[16,512]{1,0:T(8,128)} copy(f32[16,512]{1,0:T(8,128)} %direct_facet.1) | data formatting | bytes 65536

commit v4 on v3

--- a/solution.py
+++ b/solution.py
@@ -59,13 +59,13 @@
     bounds = [1]
     while bounds[-1] * 2 < plane:
         bounds.append(bounds[-1] * 2)
-    bounds += [plane * k for k in range(1, sizes[0] + 1)]
-    bounds = sorted(set(bounds))
-    return list(zip(bounds[:-1], bounds[1:]))
+    bounds.append(plane)
+    groups = list(zip(bounds[:-1], bounds[1:]))
+    return groups + [(k * plane + 1, (k + 1) * plane) for k in range(1, sizes[0])]
 
 
 def kernel(sizes, rows, vis_hbm, dest_hbm, slot_hbm, off_hbm, taper_hbm, out_ref,
-           vis_ref, dest_ref, slot_ref, off_ref, taper_ref, held, lhs, rhs, acc, load_sem, send_sem, recv_sem):
+           vis_ref, dest_ref, slot_ref, off_ref, taper_ref, held, lhs, rhs, acc, load_sem, send_sem, recv_sem, relay_sem):
     n_grp, n_au, n_vert = sizes
     count = n_grp * n_au * n_vert
     g, a, v = (lax.axis_index(name) for name in AXES)
@@ -101,7 +101,9 @@
     ]
 
     barrier = pltpu.get_barrier_semaphore()
-    for peer in peers[:0:-1]:
+    plane = n_au * n_vert
+    along = range(plane, count, plane)
+    for peer in peers[1:plane] + [peers[index] for index in along]:
         pl.semaphore_signal(barrier, inc=1, device_id=peer, device_id_type=MESH)
     for load in loads:
         load.wait()
@@ -183,19 +185,29 @@
     acc[...] = jnp.zeros_like(acc)
     fill(0, 0, held[0])
 
-    pl.semaphore_wait(barrier, count - 1)
+    pl.semaphore_wait(barrier, plane - 1 + len(along))
 
     groups = arrival_groups(sizes)
-    for number, (first, last) in reversed(list(enumerate(groups))):
-        for index in range(first, last):
-            pltpu.make_async_remote_copy(
-                src_ref=held.at[0],
-                dst_ref=held.at[index],
-                send_sem=send_sem,
-                recv_sem=recv_sem.at[number],
-                device_id=peers[index],
-                device_id_type=MESH,
-            ).start()
+
+    def send(source, index, peer, sem):
+        pltpu.make_async_remote_copy(
+            src_ref=held.at[source],
+            dst_ref=held.at[index],
+            send_sem=send_sem,
+            recv_sem=sem,
+            device_id=peer,
+            device_id_type=MESH,
+        ).start()
+
+    def spread_plane(base):
+        for number, (first, last) in enumerate(groups):
+            for index in range(first, last):
+                if base <= index < base + plane:
+                    send(base, index, peers[index - base], recv_sem.at[number])
+
+    for base in along:
+        send(0, base, peers[base], relay_sem.at[base // plane - 1])
+    spread_plane(0)
 
     def landed(first, last, sem):
         span = held.at[pl.ds(first, last - first)]
@@ -204,6 +216,11 @@
     def arrive(pair):
         for number, (first, last) in enumerate(groups):
             if first == 1:
+                continue
+
+            if isinstance(pair, int):
+                if pair == first // 2:
+                    landed(first, last, recv_sem.at[number]).wait()
                 continue
 
             @pl.when(pair == first // 2)
@@ -219,7 +236,18 @@
     landed(1, 2, recv_sem.at[0]).wait()
     fill(0, 1, held[1])
 
-    @pl.loop(0, count // 4 - 1)
+    def relay(base):
+        landed(base, base + 1, relay_sem.at[base // plane - 1]).wait()
+        spread_plane(base)
+
+    for base in along[:2]:
+        relay(base)
+    advance(1, 1)
+    for base in along[2:]:
+        relay(base)
+    advance(2, 0)
+
+    @pl.loop(1, count // 4 - 1)
     def _(quad):
         advance(2 * quad + 1, 1)
         advance(2 * quad + 2, 0)
@@ -272,6 +300,7 @@
             pltpu.SemaphoreType.DMA((5,)),
             pltpu.SemaphoreType.DMA,
             pltpu.SemaphoreType.DMA((len(arrival_groups(sizes)),)),
+            pltpu.SemaphoreType.DMA((sizes[0],)),
         ],
         compiler_params=pltpu.CompilerParams(collective_id=0, has_side_effects=True),
         name="direct_facet",

time: 17.5 us -> 18.6 us (1.063)
  Pallas kernels: 16 us -> 17 us
    pallas_call x1, Pallas kernels: 16 us -> 17 us  [body(): pl.pallas_call(functools.partial(kernel, sizes, rows), out_shape=jax.Shap...]
where the time goes in v4:
time: 18.6 us; the launch traced here: 18.4 us
  Pallas kernels  17 us (91%)
  local copies, waits for them, and re-layouts  1.38 us (7%)
    pallas_call x1, Pallas kernels, body(): pl.pallas_call(functools.partial(kernel, sizes, rows), out_shape=jax.Shap...  17 us
    unnamed x1, local copies, waits for them, and re-layouts  1.38 us

profile of v4, /device:TPU:0, one launch (start us, length us, event | category | flops | bytes accessed | tf_op | source)
XLA Modules:
  0.0 18.4 jit_solution(12401286932698841955)
XLA Ops:
  0.0 17.0 %direct_facet.1 = f32[16,512]{1,0:T(8,128)} custom-call(f32[2,256]{1,0:T(2,128)} %bitcast.4, s32[1,256]{1,0:T(1,128)} %bitcast.6, s32[1,256]{1,0:T(1,128)} %bitcast.7, s32[2,256]{1,0:T(2,128)} %bitcast.5, f32[8]{0:T(128)} %taper_hbm.1), custom_call_target="tpu_custom_call" | custom-call | tf_op jit(solution)/shard_map/direct_facet/pallas_call | solution.py:285
  17.0 1.4 %copy.7 = f32[16,512]{1,0:T(8,128)} copy(f32[16,512]{1,0:T(8,128)} %direct_facet.1) | data formatting | bytes 65536

commit v5 on v3

--- a/solution.py
+++ b/solution.py
@@ -186,7 +186,7 @@
     pl.semaphore_wait(barrier, count - 1)
 
     groups = arrival_groups(sizes)
-    for number, (first, last) in reversed(list(enumerate(groups))):
+    for number, (first, last) in enumerate(groups):
         for index in range(first, last):
             pltpu.make_async_remote_copy(
                 src_ref=held.at[0],
@@ -201,30 +201,33 @@
         span = held.at[pl.ds(first, last - first)]
         return pltpu.make_async_copy(span, span, sem)
 
-    def arrive(pair):
+    def landing(quad):
         for number, (first, last) in enumerate(groups):
-            if first == 1:
+            if first < 4:
                 continue
 
-            @pl.when(pair == first // 2)
+            @pl.when(quad == first // 4)
             def _():
                 landed(first, last, recv_sem.at[number]).wait()
 
-    def advance(pair, buffer):
-        arrive(pair)
+    def advance(quad, buffer):
+        landing(quad)
         product(1 - buffer)
-        fill(buffer, 0, held[2 * pair])
-        fill(buffer, 1, held[2 * pair + 1])
-
-    landed(1, 2, recv_sem.at[0]).wait()
-    fill(0, 1, held[1])
-
-    @pl.loop(0, count // 4 - 1)
-    def _(quad):
-        advance(2 * quad + 1, 1)
-        advance(2 * quad + 2, 0)
-
-    advance(count // 2 - 1, 1)
+        for part in range(4):
+            fill(buffer, part, held[4 * quad + part])
+
+    for number, (first, last) in enumerate(groups):
+        if first < 4:
+            landed(first, last, recv_sem.at[number]).wait()
+            for index in range(first, last):
+                fill(0, index, held[index])
+
+    @pl.loop(0, count // 8 - 1)
+    def _(step):
+        advance(2 * step + 1, 1)
+        advance(2 * step + 2, 0)
+
+    advance(count // 4 - 1, 1)
     product(1)
 
     top = blocks * pad
@@ -266,8 +269,8 @@
             pltpu.VMEM((2, vis_count), jnp.int32),
             pltpu.SMEM((SUP,), jnp.float32),
             pltpu.VMEM((count, 4, vis_count), jnp.float32),
-            pltpu.VMEM((2, 4 * (IMG // LANES) * pad, 2 * vis_count), jnp.bfloat16),
-            pltpu.VMEM((2, 2 * LANES, 2 * vis_count), jnp.bfloat16),
+            pltpu.VMEM((2, 4 * (IMG // LANES) * pad, 4 * vis_count), jnp.bfloat16),
+            pltpu.VMEM((2, 2 * LANES, 4 * vis_count), jnp.bfloat16),
             pltpu.VMEM((4 * (IMG // LANES) * pad, 2 * LANES), jnp.float32),
             pltpu.SemaphoreType.DMA((5,)),
             pltpu.SemaphoreType.DMA,

time: 17.5 us -> 17.5 us (level)
  no operation moved by 1% of the time
where the time goes in v5:
time: 17.5 us; the launch traced here: 17.3 us
  Pallas kernels  15.9 us (91%)
  local copies, waits for them, and re-layouts  1.38 us (8%)
    pallas_call x1, Pallas kernels, body(): pl.pallas_call(functools.partial(kernel, sizes, rows), out_shape=jax.Shap...  15.9 us
    unnamed x1, local copies, waits for them, and re-layouts  1.38 us

profile of v5, /device:TPU:0, one launch (start us, length us, event | category | flops | bytes accessed | tf_op | source)
XLA Modules:
  0.0 17.3 jit_solution(11895491306620140806)
XLA Ops:
  0.0 15.9 %direct_facet.1 = f32[16,512]{1,0:T(8,128)} custom-call(f32[2,256]{1,0:T(2,128)} %bitcast.4, s32[1,256]{1,0:T(1,128)} %bitcast.6, s32[1,256]{1,0:T(1,128)} %bitcast.7, s32[2,256]{1,0:T(2,128)} %bitcast.5, f32[8]{0:T(128)} %taper_hbm.1), custom_call_target="tpu_custom_call" | custom-call | tf_op jit(solution)/shard_map/direct_facet/pallas_call | solution.py:260
  15.9 1.4 %copy.7 = f32[16,512]{1,0:T(8,128)} copy(f32[16,512]{1,0:T(8,128)} %direct_facet.1) | data formatting | bytes 65536

commit v6 on v3

--- a/solution.py
+++ b/solution.py
@@ -186,7 +186,7 @@
     pl.semaphore_wait(barrier, count - 1)
 
     groups = arrival_groups(sizes)
-    for number, (first, last) in reversed(list(enumerate(groups))):
+    for number, (first, last) in enumerate(groups):
         for index in range(first, last):
             pltpu.make_async_remote_copy(
                 src_ref=held.at[0],

time: 17.5 us -> 17.2 us (0.983)
  Pallas kernels: 16 us -> 15.7 us
    pallas_call x1, Pallas kernels: 16 us -> 15.7 us  [body(): pl.pallas_call(functools.partial(kernel, sizes, rows), out_shape=jax.Shap...]
where the time goes in v6:
time: 17.2 us; the launch traced here: 17 us
  Pallas kernels  15.7 us (91%)
  local copies, waits for them, and re-layouts  1.38 us (8%)
    pallas_call x1, Pallas kernels, body(): pl.pallas_call(functools.partial(kernel, sizes, rows), out_shape=jax.Shap...  15.7 us
    unnamed x1, local copies, waits for them, and re-layouts  1.38 us

profile of v6, /device:TPU:0, one launch (start us, length us, event | category | flops | bytes accessed | tf_op | source)
XLA Modules:
  0.0 17.0 jit_solution(3031554156315439390)
XLA Ops:
  0.0 15.7 %direct_facet.1 = f32[16,512]{1,0:T(8,128)} custom-call(f32[2,256]{1,0:T(2,128)} %bitcast.4, s32[1,256]{1,0:T(1,128)} %bitcast.6, s32[1,256]{1,0:T(1,128)} %bitcast.7, s32[2,256]{1,0:T(2,128)} %bitcast.5, f32[8]{0:T(128)} %taper_hbm.1), custom_call_target="tpu_custom_call" | custom-call | tf_op jit(solution)/shard_map/direct_facet/pallas_call | solution.py:257
  15.7 1.4 %copy.7 = f32[16,512]{1,0:T(8,128)} copy(f32[16,512]{1,0:T(8,128)} %direct_facet.1) | data formatting | bytes 65536

commit v7 on v6

--- a/solution.py
+++ b/solution.py
@@ -230,12 +230,10 @@
     top = blocks * pad
     folded = acc[: 2 * top, :] + acc[2 * top :, :]
     folded = folded[:, :LANES] + folded[:, LANES:]
-    def dot(first, second):
-        return jnp.dot(
-            first, second, precision=lax.Precision.HIGHEST, preferred_element_type=jnp.float32
-        )
-
-    evens, odds = dot(folded, even), dot(folded, odd)
+    signs = jnp.concatenate([even, odd], axis=1).astype(jnp.bfloat16)
+    spread_out = jnp.dot(halves([folded]), signs, preferred_element_type=jnp.float32)
+    spread_out = spread_out[: 2 * top, :] + spread_out[2 * top :, :]
+    evens, odds = spread_out[:, :LANES], spread_out[:, LANES:]
     z_re = evens[:top, :] - odds[top:, :]
     z_im = evens[top:, :] + odds[:top, :]
     for j in range(blocks):

time: 17.2 us -> 17 us (0.988)
  Pallas kernels: 15.7 us -> 15.5 us
    pallas_call x1, Pallas kernels: 15.7 us -> 15.5 us  [body(): pl.pallas_call(functools.partial(kernel, sizes, rows), out_shape=jax.Shap...]
where the time goes in v7:
time: 17 us; the launch traced here: 16.8 us
  Pallas kernels  15.5 us (91%)
  local copies, waits for them, and re-layouts  1.38 us (8%)
    pallas_call x1, Pallas kernels, body(): pl.pallas_call(functools.partial(kernel, sizes, rows), out_shape=jax.Shap...  15.5 us
    unnamed x1, local copies, waits for them, and re-layouts  1.38 us

profile of v7, /device:TPU:0, one launch (start us, length us, event | category | flops | bytes accessed | tf_op | source)
XLA Modules:
  0.0 16.8 jit_solution(3652251514947126929)
XLA Ops:
  0.0 15.5 %direct_facet.1 = f32[16,512]{1,0:T(8,128)} custom-call(f32[2,256]{1,0:T(2,128)} %bitcast.4, s32[1,256]{1,0:T(1,128)} %bitcast.6, s32[1,256]{1,0:T(1,128)} %bitcast.7, s32[2,256]{1,0:T(2,128)} %bitcast.5, f32[8]{0:T(128)} %taper_hbm.1), custom_call_target="tpu_custom_call" | custom-call | tf_op jit(solution)/shard_map/direct_facet/pallas_call | solution.py:255
  15.5 1.4 %copy.7 = f32[16,512]{1,0:T(8,128)} copy(f32[16,512]{1,0:T(8,128)} %direct_facet.1) | data formatting | bytes 65536
